TPU v7x, 32 devices: a whole 2x2x4 slice. The times are simulated.
32 devices in a mesh: rep: 2 (over core), seq: 16 (over z, y, x).
Axes of the slice: x: 2, y: 2, z: 4, core: 2. Of those that a mesh axis runs over, the one named last changes fastest.
Arguments:
- queries: bfloat16 [4096, 8192], P(('rep', 'seq')), parts along dimension 0, may hold values from -180 to 180
- keys: bfloat16 [16384, 1024], P(('rep', 'seq')), parts along dimension 0, may hold values from -6 to 6
- values: bfloat16 [16384, 1024], P(('rep', 'seq')), parts along dimension 0, may hold values from -6 to 6
- vertical: int32 [128, 64], P('rep'), parts along dimension 0, may hold values from 0 to 127, all different within a row
- vert_count: int32 [128], P('rep'), parts along dimension 0, may hold values from 1 to 64
- slash: int32 [128, 32], P('rep'), parts along dimension 0, may hold values from 0 to 95, all different within a row
- slash_count: int32 [128], P('rep'), parts along dimension 0, may hold values from 1 to 32
Outputs:
- attended: bfloat16 [4096, 8192], P(('rep', 'seq')), parts along dimension 0
There are 2 independent parts, one for each index of `rep`. A program takes and returns all parts, laid end to end along the dimension named above; each array names one. Nothing has to cross between parts.
Inputs may be any that keep to these rules, and one draw needn't show every extreme that they name: `vertical`: each row holds 64 different key block numbers; head h uses the first vert_count[h] of them. `slash`: each row holds 32 different numbers; head h uses the first slash_count[h] of them, each number s naming the slash offset s + 1 blocks.
All inputs are finite; a program needn't handle non-finite values.
Results may differ from a plain program's by a relative error of at most 0.007.
Values may be sent and summed in bfloat16 or wider, within the bound.
No kernel may reach another device: no remote copies, remote signals or barrier semaphores. Data moves between devices by JAX's collectives and lax.ppermute only.
A program may use at most 128 MiB of HBM per device.

v0:
```python
import math
import jax
import jax.numpy as jnp
from jax import lax
from jax.sharding import PartitionSpec as P

QUERY_HEADS = 64
KV_HEADS = 8
HEAD_DIM = 128
BLOCK = 64
TURN = 4


def swapped(x, axis, bit):
    return lax.ppermute(x, axis, [(i, i ^ 1 << bit) for i in range(lax.axis_size(axis))])


def absorb(state, scores, valid, combine):
    peak, total, summed = state
    scores = jnp.where(valid, scores, -jnp.inf)
    new_peak = jnp.maximum(peak, jnp.max(scores, axis=1))
    factor = jnp.exp(peak - new_peak)
    weights = jnp.exp(scores - new_peak[:, None])
    total = total * factor + jnp.sum(weights, axis=1)
    summed = summed * factor[:, None] + combine(weights.astype(jnp.bfloat16))
    return (new_peak, total, summed)


def attend(
    query_blocks, storage, slot_of, head, first, stride, vertical, vert_count, slash, slash_count
):
    count_rows, block, width = query_blocks.shape
    total_blocks = storage.shape[0] // block
    cache = storage.reshape(total_blocks, block, 2 * width)
    scale = 1.0 / math.sqrt(width)
    rows = count_rows * block
    absolute = (
        total_blocks
        - count_rows * stride
        + first
        + stride * jnp.arange(count_rows, dtype=jnp.int32)
    )
    verticals = vertical[head]
    live_vert = vert_count[head]
    offsets = slash[head] + 1
    live_slash = slash_count[head]
    lanes = jnp.arange(TURN, dtype=jnp.int32)
    marks = jnp.arange(verticals.shape[0], dtype=jnp.int32) < live_vert
    flat_query = query_blocks.reshape(rows, width)
    diagonal = cache[slot_of(absolute)]
    scores = (
        jnp.einsum(
            "rqd,rkd->rqk", query_blocks, diagonal[:, :, :width], preferred_element_type=jnp.float32
        )
        * scale
    )
    causal = jnp.arange(block)[:, None] >= jnp.arange(block)[None, :]
    scores = jnp.where(causal[None], scores, -jnp.inf)
    peak = jnp.max(scores, axis=2)
    weights = jnp.exp(scores - peak[:, :, None])
    total = jnp.sum(weights, axis=2)
    summed = jnp.einsum(
        "rqk,rkd->rqd",
        weights.astype(jnp.bfloat16),
        diagonal[:, :, width:],
        preferred_element_type=jnp.float32,
    )
    state = (peak.reshape(rows), total.reshape(rows), summed.reshape(rows, width))

    def widen(usable):
        return jnp.broadcast_to(usable[:, None, :, None], (count_rows, block, TURN, block)).reshape(
            rows, TURN * block
        )

    def vertical_turn(step, state):
        picked = lax.dynamic_slice_in_dim(verticals, step * TURN, TURN)
        keys_here = cache[slot_of(picked)].reshape(TURN * block, 2 * width)
        scores = (
            lax.dot_general(
                flat_query,
                keys_here[:, :width],
                (((1,), (1,)), ((), ())),
                preferred_element_type=jnp.float32,
            )
            * scale
        )
        usable = (step * TURN + lanes < live_vert)[None, :] & (picked[None, :] < absolute[:, None])

        def combine(rounded):
            return jnp.dot(rounded, keys_here[:, width:], preferred_element_type=jnp.float32)

        return absorb(state, scores, widen(usable), combine)

    state = lax.fori_loop(0, (live_vert + TURN - 1) // TURN, vertical_turn, state)

    def slash_turn(step, state):
        picked = lax.dynamic_slice_in_dim(offsets, step * TURN, TURN)
        target = absolute[:, None] - picked[None, :]
        keys_here = cache[slot_of(target)].reshape(count_rows, TURN * block, 2 * width)
        scores = (
            jnp.einsum(
                "rqd,rkd->rqk",
                query_blocks,
                keys_here[:, :, :width],
                preferred_element_type=jnp.float32,
            ).reshape(rows, TURN * block)
            * scale
        )
        covered = jnp.any(
            (target[:, :, None] == verticals[None, None, :]) & marks[None, None, :], axis=2
        )
        usable = (step * TURN + lanes < live_slash)[None, :] & jnp.logical_not(covered)

        def combine(rounded):
            return jnp.einsum(
                "rqk,rkd->rqd",
                rounded.reshape(count_rows, block, TURN * block),
                keys_here[:, :, width:],
                preferred_element_type=jnp.float32,
            ).reshape(rows, width)

        return absorb(state, scores, widen(usable), combine)

    state = lax.fori_loop(0, (live_slash + TURN - 1) // TURN, slash_turn, state)
    peak, total, summed = state
    return (summed / total[:, None]).astype(jnp.bfloat16).reshape(count_rows, block, width)


def body(queries, keys, values, vertical, vert_count, slash, slash_count):
    seq_count = lax.axis_size("seq")
    position = lax.axis_index("seq")
    query_rows = queries.shape[0]
    key_rows = keys.shape[0]
    group_devices = seq_count // KV_HEADS
    local_cache = jnp.concatenate(
        [keys.reshape(key_rows, KV_HEADS, HEAD_DIM), values.reshape(key_rows, KV_HEADS, HEAD_DIM)],
        axis=2,
    )
    piece_rows = key_rows // group_devices
    pieces = (
        local_cache.reshape(group_devices, piece_rows, KV_HEADS, 2 * HEAD_DIM)
        .transpose(1, 2, 0, 3)
        .reshape(piece_rows, seq_count, 2 * HEAD_DIM)
    )
    stacked = lax.all_to_all(pieces, "seq", split_axis=1, concat_axis=0, tiled=True).reshape(
        1, seq_count * piece_rows, 2 * HEAD_DIM
    )
    for level in range(group_devices.bit_length() - 1):
        partner = swapped(stacked, "seq", level)
        upper_side = position // 2**level % 2 == 1
        lower = jnp.where(upper_side, partner, stacked)
        upper = jnp.where(upper_side, stacked, partner)
        stacked = jnp.concatenate([lower, upper], axis=0)
    storage = stacked.reshape(group_devices * seq_count * piece_rows, 2 * HEAD_DIM)
    device_blocks = key_rows // BLOCK
    piece_blocks = piece_rows // BLOCK

    def slot_of(index):
        sender = index // device_blocks
        within = index % device_blocks
        return (
            within // piece_blocks * (seq_count * piece_blocks)
            + sender * piece_blocks
            + within % piece_blocks
        )

    per_device = QUERY_HEADS // seq_count
    blocks = queries.reshape(query_rows // BLOCK, BLOCK, QUERY_HEADS, HEAD_DIM)
    gathered = lax.all_to_all(blocks, "seq", split_axis=2, concat_axis=0, tiled=True)
    results = []
    for local in range(per_device):
        results.append(
            attend(
                gathered[:, :, local, :],
                storage,
                slot_of,
                position * per_device + local,
                0,
                1,
                vertical,
                vert_count,
                slash,
                slash_count,
            )
        )
    answer = lax.all_to_all(
        jnp.stack(results, axis=2), "seq", split_axis=0, concat_axis=2, tiled=True
    )
    return answer.reshape(query_rows, QUERY_HEADS * HEAD_DIM)


def solution(mesh):
    return jax.shard_map(
        body,
        mesh=mesh,
        in_specs=(
            P(("rep", "seq"), None),
            P(("rep", "seq"), None),
            P(("rep", "seq"), None),
            P("rep", None),
            P("rep"),
            P("rep", None),
            P("rep"),
        ),
        out_specs=P(("rep", "seq"), None),
        check_vma=False,
    )
```

profile of v0, /device:TPU:0, one launch (start us, length us, event | category | flops | bytes accessed | tf_op | source)
XLA Modules:
  0.0 1188.1 jit_solution(315355499021703888)
XLA Ops:
  3.9 8.3 all-to-all-start
  17.1 38.2 %all-to-all-done = bf16[256,16,256]{2,0,1:T(8,128)(2,1)S(1)} async-done(((bf16[256,16,256]{2,0,1:T(8,128)(2,1)}), bf16[256,16,256]{2,0,1:T(8,128)(2,1)S(1)}, u32[]{:S(2)}, u32[]{:S(2)}) %all-to-all-start) | async-done | bytes 2097184 | tf_op jit(solution)/shard_map/all_to_all | solution.py:145
  56.6 10.0 all-to-all-start.1
  76.7 32.6 %all-to-all-done.1 = bf16[2,64,64,128]{3,1,0,2:T(8,128)(2,1)S(1)} async-done(((bf16[2,64,64,128]{3,1,0,2:T(8,128)(2,1)}), bf16[2,64,64,128]{3,1,0,2:T(8,128)(2,1)S(1)}, u32[]{:S(2)}, u32[]{:S(2)}) %all-to-all-start.1) | async-done | bytes 2097184 | tf_op jit(solution)/shard_map/all_to_all | solution.py:169
  112.2 23.4 %collective-permute-done = bf16[1,4096,256]{2,1,0:T(8,128)(2,1)} collective-permute-done((bf16[1,4096,256]{2,1,0:T(8,128)(2,1)}, bf16[1,4096,256]{2,1,0:T(8,128)(2,1)}, u32[]{:S(2)}, u32[]{:S(2)}) %collective-permute-start) | collective-permute-done | bytes 2097184 | tf_op jit(solution)/shard_map/ppermute | solution.py:15
  155.0 12.7 %while.148 = (s32[]{:T(128)}, f32[2048]{0:T(1024)S(1)}, f32[2048]{0:T(1024)S(1)}, f32[2048,128]{1,0:T(8,128)S(1)}, s32[]{:T(128)}, /*index=5*/s32[]{:T(128)}, s3...) while((s32[]{:T(128)}, f32[2048]{0:T(1024)S(1)}, ...), condition=%wide.region_5.6_spmd.clone, body=%wide.region_2.5_spmd.clone.sunk | while | flops 272635360 | bytes 11539231 | solution.py:94
  157.7 4.2 reshape.1859
  167.7 126.9 %while.152 = (s32[]{:T(128)}, f32[2048]{0:T(1024)S(1)}, f32[2048]{0:T(1024)S(1)}, f32[2048,128]{1,0:T(8,128)S(1)}, s32[]{:T(128)}, /*index=5*/s32[]{:T(128)}, s3...) while((s32[]{:T(128)}, f32[2048]{0:T(1024)S(1)}, ...), condition=%wide.region_10.11_spmd.clone.clone, body=%wide.region_6.10_spmd.clone.clone.sunk | while | flops 274762880 | bytes 32220464 | solution.py:124
  170.1 5.0 gather_fusion
  188.2 5.0 gather_fusion
  206.3 5.0 gather_fusion
  224.5 5.0 gather_fusion
  242.6 5.0 gather_fusion
  260.7 5.0 gather_fusion
  278.8 5.0 gather_fusion
  295.7 195.0 %while.149 = (s32[]{:T(128)}, f32[2048]{0:T(1024)S(1)}, f32[2048]{0:T(1024)S(1)}, f32[2048,128]{1,0:T(8,128)S(1)}, s32[]{:T(128)}, /*index=5*/s32[]{:T(128)}, s3...) while((s32[]{:T(128)}, f32[2048]{0:T(1024)S(1)}, ...), condition=%wide.region_16.17_spmd.clone, body=%wide.region_13.16_spmd.clone.sunk | while | flops 272635360 | bytes 11539231 | solution.py:94
  297.8 4.2 reshape.1862
  310.0 4.2 reshape.1862
  322.2 4.2 reshape.1862
  334.4 4.2 reshape.1862
  346.6 4.2 reshape.1862
  358.8 4.2 reshape.1862
  371.0 4.2 reshape.1862
  383.1 4.2 reshape.1862
  395.3 4.2 reshape.1862
  490.7 125.9 %while.153 = (s32[]{:T(128)}, f32[2048]{0:T(1024)S(1)}, f32[2048]{0:T(1024)S(1)}, f32[2048,128]{1,0:T(8,128)S(1)}, s32[]{:T(128)}, /*index=5*/s32[]{:T(128)}, s3...) while((s32[]{:T(128)}, f32[2048]{0:T(1024)S(1)}, ...), condition=%wide.region_21.22_spmd.clone.clone, body=%wide.region_17.21_spmd.clone.clone.sunk | while | flops 274762880 | bytes 34317640 | solution.py:124
  493.1 5.0 gather_fusion.1
  508.8 5.0 gather_fusion.1
  524.6 5.0 gather_fusion.1
  540.3 5.0 gather_fusion.1
  556.0 5.0 gather_fusion.1
  571.7 5.0 gather_fusion.1
  587.4 5.0 gather_fusion.1
  603.1 5.0 gather_fusion.1
  616.7 81.9 %while.150 = (s32[]{:T(128)}, f32[2048]{0:T(1024)S(1)}, f32[2048]{0:T(1024)S(1)}, f32[2048,128]{1,0:T(8,128)S(1)}, s32[]{:T(128)}, /*index=5*/s32[]{:T(128)}, s3...) while((s32[]{:T(128)}, f32[2048]{0:T(1024)S(1)}, ...), condition=%wide.region_27.28_spmd.clone, body=%wide.region_24.27_spmd.clone.sunk | while | flops 272635360 | bytes 11539231 | solution.py:94
  698.7 126.0 %while.154 = (s32[]{:T(128)}, f32[2048]{0:T(1024)S(1)}, f32[2048]{0:T(1024)S(1)}, f32[2048,128]{1,0:T(8,128)S(1)}, s32[]{:T(128)}, /*index=5*/s32[]{:T(128)}, s3...) while((s32[]{:T(128)}, f32[2048]{0:T(1024)S(1)}, ...), condition=%wide.region_32.33_spmd.clone.clone, body=%wide.region_28.32_spmd.clone.clone.sunk | while | flops 274762880 | bytes 32220464 | solution.py:124
  701.1 5.0 gather_fusion.2
  719.1 5.0 gather_fusion.2
  737.1 5.0 gather_fusion.2
  755.0 5.0 gather_fusion.2
  773.0 5.0 gather_fusion.2
  791.0 5.0 gather_fusion.2
  809.0 5.0 gather_fusion.2
  824.8 61.2 %while.151 = (s32[]{:T(128)}, f32[2048]{0:T(1024)S(1)}, f32[2048]{0:T(1024)S(1)}, f32[2048,128]{1,0:T(8,128)S(1)}, s32[]{:T(128)}, /*index=5*/s32[]{:T(128)}, s3...) while((s32[]{:T(128)}, f32[2048]{0:T(1024)S(1)}, ...), condition=%wide.region_38.39_spmd.clone, body=%wide.region_35.38_spmd.clone.sunk | while | flops 272635360 | bytes 11539231 | solution.py:94
  886.0 35.8 %while.155 = (s32[]{:T(128)}, f32[2048]{0:T(1024)S(1)}, f32[2048]{0:T(1024)S(1)}, f32[2048,128]{1,0:T(8,128)S(1)}, s32[]{:T(128)}, /*index=5*/s32[]{:T(128)}, s3...) while((s32[]{:T(128)}, f32[2048]{0:T(1024)S(1)}, ...), condition=%wide.region_43.44_spmd.clone.clone, body=%wide.region_39.43_spmd.clone.clone.sunk | while | flops 274762880 | bytes 32220464 | solution.py:124
  888.3 5.0 gather_fusion.3
  906.2 5.0 gather_fusion.3
  924.7 258.7 %all_to_all.48 = bf16[32,64,4,128]{3,1,2,0:T(8,128)(2,1)S(1)} all-to-all(bf16[32,64,4,128]{3,1,2,0:T(8,128)(2,1)S(1)} %pad_maximum_fusion.1), channel_id=1, replica_groups=mesh['rep'=2,'seq'=16] {'seq'}, dimensions={0} | all-to-all | bytes 4194304 | tf_op jit(solution)/shard_map/all_to_all | solution.py:186
  (1105 shorter events, 643.5 us)
Async XLA Ops:
  3.9 51.4 %all-to-all-start = ((bf16[256,16,256]{2,0,1:T(8,128)(2,1)}), bf16[256,16,256]{2,0,1:T(8,128)(2,1)S(1)}, u32[]{:S(2)}, u32[]{:S(2)}) async-start(bf16[256,16,256]{2,0,1:T(8,128)(2,1)} %bitcast.1), calls=%async_computation | async-start | bytes 4194304 | tf_op jit(solution)/shard_map/all_to_all | solution.py:145
  17.1 51.5 %copy-start.19 = (s32[64]{0:T(128)S(1)}, s32[64]{0:T(128)}, u32[]{:S(2)}) copy-start(s32[64]{0:T(128)} %param.29) | copy-start | bytes 772
  17.1 51.5 %copy-start.20 = (s32[64]{0:T(128)S(1)}, s32[64]{0:T(128)}, u32[]{:S(2)}) copy-start(s32[64]{0:T(128)} %param.27) | copy-start | bytes 772
  17.1 57.3 %copy-start.16 = (s32[64,32]{0,1:T(8,128)S(1)}, s32[64,32]{0,1:T(8,128)}, u32[]{:S(2)}) copy-start(s32[64,32]{0,1:T(8,128)} %param.28) | copy-start | bytes 24580
  56.6 52.6 %all-to-all-start.1 = ((bf16[2,64,64,128]{3,1,0,2:T(8,128)(2,1)}), bf16[2,64,64,128]{3,1,0,2:T(8,128)(2,1)S(1)}, u32[]{:S(2)}, u32[]{:S(2)}) async-start(bf16[2,64,64,128]{3,1,0,2:T(8,128)(2,1)} %copy.39), calls=%async_computation.1 | async-start | bytes 4194304 | tf_op jit(solution)/shard_map/all_to_all | solution.py:169
  66.7 69.0 %collective-permute-start = (bf16[1,4096,256]{2,1,0:T(8,128)(2,1)}, bf16[1,4096,256]{2,1,0:T(8,128)(2,1)}, u32[]{:S(2)}, u32[]{:S(2)}) collective-permute-start(bf16[1,4096,256]{2,1,0:T(8,128)(2,1)} %bitcast.307), channel_id=1, source_target_pairs={{0,1},{1,0},{2,3},{3,2},{4,5},{5,4},{6,7},{7,6},{8,9},{9,8},{10,11... | collective-permute-start | bytes 6291464 | tf_op jit(solution)/shard_map/ppermute | solution.py:15
  109.4 2.8 copy-start.8
  109.5 26.2 %copy-start.10 = (bf16[256,16,256]{2,0,1:T(8,128)(2,1)S(1)}, bf16[256,16,256]{2,0,1:T(8,128)(2,1)}, u32[]{:S(2)}) copy-start(bf16[256,16,256]{2,0,1:T(8,128)(2,1)} %copy-done.9) | copy-start | bytes 6291460
  142.7 4.6 copy-start.6
  150.4 1.7 copy-start.7
  179.1 4.1 copy-start.2
  197.2 4.1 copy-start.2
  215.3 4.1 copy-start.2
  233.4 4.1 copy-start.2
  251.6 4.1 copy-start.2
  269.7 4.1 copy-start.2
  287.8 4.1 copy-start.2
  493.1 5.0 copy-start.15
  502.1 3.0 copy-start.3
  508.8 5.0 copy-start.15
  517.8 3.0 copy-start.3
  524.6 5.0 copy-start.15
  533.5 3.0 copy-start.3
  540.3 5.0 copy-start.15
  549.2 3.0 copy-start.3
  556.0 5.0 copy-start.15
  564.9 3.0 copy-start.3
  571.7 5.0 copy-start.15
  580.7 3.0 copy-start.3
  587.4 5.0 copy-start.15
  596.4 3.0 copy-start.3
  603.1 5.0 copy-start.15
  612.1 3.0 copy-start.3
  698.6 126.0 %copy-start.17 = (f32[32,64]{1,0:T(8,128)S(1)}, f32[32,64]{1,0:T(8,128)}, u32[]{:S(2)}) copy-start(f32[32,64]{1,0:T(8,128)} %fusion.203) | copy-start | bytes 24580
  698.6 126.1 %copy-start = (f32[32,64,128]{2,1,0:T(8,128)S(1)}, f32[32,64,128]{2,1,0:T(8,128)}, u32[]{:S(2)}) copy-start(f32[32,64,128]{2,1,0:T(8,128)} %fusion.204) | copy-start | bytes 3145732
  698.7 126.1 %copy-start.11 = (f32[2048]{0:T(1024)S(1)}, f32[2048]{0:T(1024)}, u32[]{:S(2)}) copy-start(f32[2048]{0:T(1024)} %reshape.1697) | copy-start | bytes 24580
  698.7 126.1 %copy-start.18 = (s32[1,64]{1,0:T(1,128)S(1)}, s32[1,64]{1,0:T(1,128)}, u32[]{:S(2)}) copy-start(s32[1,64]{1,0:T(1,128)} %get-tuple-element.2841) | copy-start | bytes 772
  710.1 4.0 copy-start.4
  728.0 4.0 copy-start.4
  746.0 4.0 copy-start.4
  764.0 4.0 copy-start.4
  782.0 4.0 copy-start.4
  800.0 4.0 copy-start.4
  818.0 4.0 copy-start.4
  824.8 61.2 %copy-start.21 = (s32[32]{0:T(128)S(1)}, s32[32]{0:T(128)}, u32[]{:S(2)}) copy-start(s32[32]{0:T(128)} %get-tuple-element.2840) | copy-start | bytes 388
  886.0 35.8 %copy-start.13 = (f32[2048]{0:T(1024)S(1)}, f32[2048]{0:T(1024)}, u32[]{:S(2)}) copy-start(f32[2048]{0:T(1024)} %copy-done.12) | copy-start | bytes 24580
  897.2 4.0 copy-start.5
  915.1 4.0 copy-start.5
  (4 other events, 5.1 us)
where the time goes:
time: 1200 us; the launch traced here: 1190 us
  local copies, waits for them, and re-layouts  393 us (33%)
  matrix products  271 us (23%)
  blocking collectives  259 us (22%)
  other arithmetic  139 us (12%)
  waiting for transfers between devices  94.2 us (8%)
  starting transfers between devices  20.3 us (2%)
    all_to_all x1, blocking collectives, body(): lax.all_to_all(jnp.stack(results, axis=2), 'seq', split_axis=0, concat_ax...  259 us
    gather x24, local copies, waits for them, and re-layouts, slash_turn(): cache[slot_of(target)].reshape(count_rows, TURN * block, 2 * width)  120 us
    reshape x30, local copies, waits for them, and re-layouts, widen(): jnp.broadcast_to(usable[:, None, :, None], (count_rows, block, TURN, block))  118 us
    dot_general x24, matrix products, slash_turn(): jnp.einsum('rqd,rkd->rqk', query_blocks, keys_here[:, :, :width], preferr...  91.6 us
    dot_general x24, matrix products, combine(): jnp.einsum('rqk,rkd->rqd', rounded.reshape(count_rows, block, TURN * bloc...  88.2 us
    gather x30, local copies, waits for them, and re-layouts, vertical_turn(): keys_here = cache[slot_of(picked)].reshape(TURN * block, 2 * width)  82.2 us
    dot_general x30, matrix products, vertical_turn(): lax.dot_general(flat_query, keys_here[:, :width], (((1,), (1,)), ((), ())...  51.4 us
    all_to_all x1, waiting for transfers between devices, body(): lax.all_to_all(pieces, 'seq', split_axis=1, concat_axis=0, tiled=True)  38.2 us
  transfers between devices with their start and end apart: 3, of which 3 were waited for; matrix products, arithmetic and copies ran while one was open for 1% of the time, Pallas kernels for 0%

commit v1 on v0

--- a/solution.py
+++ b/solution.py
@@ -9,6 +9,30 @@
 HEAD_DIM = 128
 BLOCK = 64
 TURN = 4
+
+
+def cut_along(x, dim, length):
+    shape = x.shape
+    tiles = x.reshape(*shape[:dim], length, shape[dim] // length, *shape[dim + 1 :])
+    return jnp.moveaxis(tiles, dim, 0)
+
+
+def in_order(parts, dim):
+    parts = jnp.moveaxis(parts, 0, dim)
+    shape = parts.shape
+    return parts.reshape(*shape[:dim], shape[dim] * shape[dim + 1], *shape[dim + 2 :])
+
+
+def sent_to_each(shard, axis, split_dim, concat_dim):
+    size, index = (lax.axis_size(axis), lax.axis_index(axis))
+    parts = cut_along(shard, split_dim, size)
+    whole = parts
+    for step in range(1, size):
+        target, source = ((index + step) % size, (index - step) % size)
+        sent = lax.dynamic_index_in_dim(parts, target, 0)
+        theirs = lax.ppermute(sent, axis, [(i, (i + step) % size) for i in range(size)])
+        whole = lax.dynamic_update_slice_in_dim(whole, theirs, source, axis=0)
+    return in_order(whole, concat_dim)
 
 
 def swapped(x, axis, bit):
@@ -183,9 +207,7 @@
                 slash_count,
             )
         )
-    answer = lax.all_to_all(
-        jnp.stack(results, axis=2), "seq", split_axis=0, concat_axis=2, tiled=True
-    )
+    answer = sent_to_each(jnp.stack(results, axis=2), "seq", 0, 2)
     return answer.reshape(query_rows, QUERY_HEADS * HEAD_DIM)
 
 

time: 1200 us -> 1100 us (0.917)
  blocking collectives: 259 us -> 0 us
  starting transfers between devices: 20.3 us -> 236 us
  local copies, waits for them, and re-layouts: 393 us -> 356 us
  matrix products: 271 us -> 237 us
    all_to_all x1 -> x0, blocking collectives: 259 us -> none  [body(): lax.all_to_all(jnp.stack(results, axis=2), 'seq', split_axis=0, concat_ax...]
    ppermute x0 -> x15, starting transfers between devices: none -> 216 us  [sent_to_each(): lax.ppermute(sent, axis, [(i, (i + step) % size) for i in range(size)])]
    reshape x30, local copies, waits for them, and re-layouts: 118 us -> 88.7 us  [widen(): jnp.broadcast_to(usable[:, None, :, None], (count_rows, block, TURN, block))]
    broadcast_in_dim x78, local copies, waits for them, and re-layouts: 36.3 us -> 15.9 us  [widen(): jnp.broadcast_to(usable[:, None, :, None], (count_rows, block, TURN, block))]
    dot_general x30, matrix products: 51.4 us -> 35.7 us  [vertical_turn(): lax.dot_general(flat_query, keys_here[:, :width], (((1,), (1,)), ((), ())...]
    ppermute x0 -> x15, waiting for transfers between devices: none -> 12.7 us  [sent_to_each(): lax.ppermute(sent, axis, [(i, (i + step) % size) for i in range(size)])]
  transfers between devices with their start and end apart: 3 -> 18, of which waited for: 3 -> 7; matrix products, arithmetic and copies ran while one was open for 1% -> 1% of each run, Pallas kernels for 0% -> 0%
where the time goes in v1:
time: 1100 us; the launch traced here: 1090 us
  local copies, waits for them, and re-layouts  356 us (32%)
  matrix products  237 us (22%)
  starting transfers between devices  236 us (21%)
  other arithmetic  140 us (13%)
  waiting for transfers between devices  104 us (9%)
    ppermute x15, starting transfers between devices, sent_to_each(): lax.ppermute(sent, axis, [(i, (i + step) % size) for i in range(size)])  216 us
    gather x24, local copies, waits for them, and re-layouts, slash_turn(): cache[slot_of(target)].reshape(count_rows, TURN * block, 2 * width)  120 us
    reshape x30, local copies, waits for them, and re-layouts, widen(): jnp.broadcast_to(usable[:, None, :, None], (count_rows, block, TURN, block))  88.7 us
    dot_general x24, matrix products, slash_turn(): jnp.einsum('rqd,rkd->rqk', query_blocks, keys_here[:, :, :width], preferr...  82.7 us
    gather x30, local copies, waits for them, and re-layouts, vertical_turn(): keys_here = cache[slot_of(picked)].reshape(TURN * block, 2 * width)  82.2 us
    dot_general x24, matrix products, combine(): jnp.einsum('rqk,rkd->rqd', rounded.reshape(count_rows, block, TURN * bloc...  80 us
    all_to_all x1, waiting for transfers between devices, body(): lax.all_to_all(pieces, 'seq', split_axis=1, concat_axis=0, tiled=True)  38.2 us
    dot_general x30, matrix products, vertical_turn(): lax.dot_general(flat_query, keys_here[:, :width], (((1,), (1,)), ((), ())...  35.7 us
  transfers between devices with their start and end apart: 18, of which 7 were waited for; matrix products, arithmetic and copies ran while one was open for 1% of the time, Pallas kernels for 0%

profile of v1, /device:TPU:0, one launch (start us, length us, event | category | flops | bytes accessed | tf_op | source)
XLA Modules:
  0.0 1086.3 jit_solution(1096041139637235611)
XLA Ops:
  3.9 8.3 all-to-all-start
  17.1 38.2 %all-to-all-done = bf16[256,16,256]{2,0,1:T(8,128)(2,1)S(1)} async-done(((bf16[256,16,256]{2,0,1:T(8,128)(2,1)}), bf16[256,16,256]{2,0,1:T(8,128)(2,1)S(1)}, u32[]{:S(2)}, u32[]{:S(2)}) %all-to-all-start) | async-done | bytes 2097184 | tf_op jit(solution)/shard_map/all_to_all | solution.py:169
  56.6 10.0 all-to-all-start.1
  76.7 32.6 %all-to-all-done.1 = bf16[2,64,64,128]{3,1,0,2:T(8,128)(2,1)S(1)} async-done(((bf16[2,64,64,128]{3,1,0,2:T(8,128)(2,1)}), bf16[2,64,64,128]{3,1,0,2:T(8,128)(2,1)S(1)}, u32[]{:S(2)}, u32[]{:S(2)}) %all-to-all-start.1) | async-done | bytes 2097184 | tf_op jit(solution)/shard_map/all_to_all | solution.py:193
  115.1 20.6 %collective-permute-done = bf16[1,4096,256]{2,1,0:T(8,128)(2,1)} collective-permute-done((bf16[1,4096,256]{2,1,0:T(8,128)(2,1)}, bf16[1,4096,256]{2,1,0:T(8,128)(2,1)}, u32[]{:S(2)}, u32[]{:S(2)}) %collective-permute-start) | collective-permute-done | bytes 2097184 | tf_op jit(solution)/shard_map/ppermute | solution.py:39
  153.7 12.4 %while.148 = (s32[]{:T(128)}, f32[2048]{0:T(1024)S(1)}, f32[2048]{0:T(1024)S(1)}, f32[2048,128]{1,0:T(8,128)S(1)}, s32[]{:T(128)}, /*index=5*/s32[]{:T(128)}, s3...) while((s32[]{:T(128)}, f32[2048]{0:T(1024)S(1)}, ...), condition=%wide.region_5.6_spmd.clone, body=%wide.region_2.5_spmd.clone.sunk | while | flops 272635360 | bytes 11539231 | solution.py:118
  156.1 4.2 reshape.1863
  166.1 126.2 %while.152 = (s32[]{:T(128)}, f32[2048]{0:T(1024)S(1)}, f32[2048]{0:T(1024)S(1)}, f32[2048,128]{1,0:T(8,128)S(1)}, s32[]{:T(128)}, /*index=5*/s32[]{:T(128)}, s3...) while((s32[]{:T(128)}, f32[2048]{0:T(1024)S(1)}, ...), condition=%wide.region_10.11_spmd.clone.clone, body=%wide.region_6.10_spmd.clone.clone.sunk | while | flops 274762880 | bytes 32220464 | solution.py:148
  168.5 5.0 gather_fusion
  186.5 5.0 gather_fusion
  195.5 4.0 fusion.329
  204.5 5.0 gather_fusion
  213.5 4.0 fusion.329
  222.6 5.0 gather_fusion
  240.6 5.0 gather_fusion
  258.6 5.0 gather_fusion
  276.7 5.0 gather_fusion
  294.6 163.6 %while.149 = (s32[]{:T(128)}, f32[2048]{0:T(1024)S(1)}, f32[2048]{0:T(1024)S(1)}, f32[2048,128]{1,0:T(8,128)S(1)}, s32[]{:T(128)}, /*index=5*/s32[]{:T(128)}, s3...) while((s32[]{:T(128)}, f32[2048]{0:T(1024)S(1)}, ...), condition=%wide.region_16.17_spmd.clone, body=%wide.region_13.16_spmd.clone.sunk | while | flops 272635360 | bytes 11539231 | solution.py:118
  458.1 125.9 %while.153 = (s32[]{:T(128)}, f32[2048]{0:T(1024)S(1)}, f32[2048]{0:T(1024)S(1)}, f32[2048,128]{1,0:T(8,128)S(1)}, s32[]{:T(128)}, /*index=5*/s32[]{:T(128)}, s3...) while((s32[]{:T(128)}, f32[2048]{0:T(1024)S(1)}, ...), condition=%wide.region_21.22_spmd.clone.clone, body=%wide.region_17.21_spmd.clone.clone.sunk | while | flops 274762880 | bytes 34317640 | solution.py:148
  460.6 5.0 gather_fusion.1
  476.3 5.0 gather_fusion.1
  492.0 5.0 gather_fusion.1
  507.7 5.0 gather_fusion.1
  523.5 5.0 gather_fusion.1
  539.2 5.0 gather_fusion.1
  554.9 5.0 gather_fusion.1
  570.6 5.0 gather_fusion.1
  586.3 67.3 %while.150 = (s32[]{:T(128)}, f32[2048]{0:T(1024)S(1)}, f32[2048]{0:T(1024)S(1)}, f32[2048,128]{1,0:T(8,128)S(1)}, s32[]{:T(128)}, /*index=5*/s32[]{:T(128)}, s3...) while((s32[]{:T(128)}, f32[2048]{0:T(1024)S(1)}, ...), condition=%wide.region_27.28_spmd.clone, body=%wide.region_24.27_spmd.clone.sunk | while | flops 272635360 | bytes 11539231 | solution.py:118
  653.6 111.4 %while.154 = (s32[]{:T(128)}, f32[2048]{0:T(1024)S(1)}, f32[2048]{0:T(1024)S(1)}, f32[2048,128]{1,0:T(8,128)S(1)}, s32[]{:T(128)}, /*index=5*/s32[]{:T(128)}, s3...) while((s32[]{:T(128)}, f32[2048]{0:T(1024)S(1)}, ...), condition=%wide.region_32.33_spmd.clone.clone, body=%wide.region_28.32_spmd.clone.clone.sunk | while | flops 274762880 | bytes 23831828 | solution.py:148
  655.9 5.0 gather_fusion.2
  671.8 5.0 gather_fusion.2
  687.8 5.0 gather_fusion.2
  703.7 5.0 gather_fusion.2
  719.6 5.0 gather_fusion.2
  735.5 5.0 gather_fusion.2
  751.4 5.0 gather_fusion.2
  767.3 42.5 %while.151 = (s32[]{:T(128)}, f32[2048]{0:T(1024)S(1)}, f32[2048]{0:T(1024)S(1)}, f32[2048,128]{1,0:T(8,128)S(1)}, s32[]{:T(128)}, /*index=5*/s32[]{:T(128)}, s3...) while((s32[]{:T(128)}, f32[2048]{0:T(1024)S(1)}, ...), condition=%wide.region_38.39_spmd.clone, body=%wide.region_35.38_spmd.clone.sunk | while | flops 272635360 | bytes 11539231 | solution.py:118
  809.8 31.4 %while.155 = (s32[]{:T(128)}, f32[2048]{0:T(1024)S(1)}, f32[2048]{0:T(1024)S(1)}, f32[2048,128]{1,0:T(8,128)S(1)}, s32[]{:T(128)}, /*index=5*/s32[]{:T(128)}, s3...) while((s32[]{:T(128)}, f32[2048]{0:T(1024)S(1)}, ...), condition=%wide.region_43.44_spmd.clone.clone, body=%wide.region_39.43_spmd.clone.clone.sunk | while | flops 274762880 | bytes 34317640 | solution.py:148
  812.0 5.0 gather_fusion.3
  827.7 5.0 gather_fusion.3
  843.1 4.9 pad_maximum_fusion.1
  848.3 8.4 collective-permute-done.1
  859.6 9.5 collective-permute-start.2
  869.1 160.6 %collective-permute-start.3 = (bf16[1,2,64,4,128]{4,3,0,2,1:T(4,128)(2,1)}, bf16[1,2,64,4,128]{4,3,0,2,1:T(4,128)(2,1)}, u32[]{:S(2)}, u32[]{:S(2)}) collective-permute-start(bf16[1,2,64,4,128]{4,3,0,2,1:T(4,128)(2,1)} %get-tuple-element.2199), channel_id=1, source_target_pairs={{0,3},{1,4},{2,5},{3,6},{4,7},{5,8},{6,9},{7,10},{8,11},{9,12},{10... | collective-permute-start | bytes 393224 | tf_op jit(solution)/shard_map/ppermute | solution.py:33
  1029.7 11.8 %collective-permute-start.4 = (bf16[1,2,64,4,128]{4,3,0,2,1:T(4,128)(2,1)}, bf16[1,2,64,4,128]{4,3,0,2,1:T(4,128)(2,1)S(1)}, u32[]{:S(2)}, u32[]{:S(2)}) collective-permute-start(bf16[1,2,64,4,128]{4,3,0,2,1:T(4,128)(2,1)} %get-tuple-element.2198), channel_id=1, source_target_pairs={{0,4},{1,5},{2,6},{3,7},{4,8},{5,9},{6,10},{7,11},{8,12},{9,13},{1... | collective-permute-start | bytes 393224 | tf_op jit(solution)/shard_map/ppermute | solution.py:33
  1041.9 6.7 collective-permute-start.7
  1055.4 9.5 collective-permute-start.10
  1073.9 4.1 collective-permute-start.14
  (1149 shorter events, 616.7 us)
Async XLA Ops:
  3.9 51.4 %all-to-all-start = ((bf16[256,16,256]{2,0,1:T(8,128)(2,1)}), bf16[256,16,256]{2,0,1:T(8,128)(2,1)S(1)}, u32[]{:S(2)}, u32[]{:S(2)}) async-start(bf16[256,16,256]{2,0,1:T(8,128)(2,1)} %bitcast.1), calls=%async_computation | async-start | bytes 4194304 | tf_op jit(solution)/shard_map/all_to_all | solution.py:169
  17.1 51.5 %copy-start.22 = (s32[64]{0:T(128)S(1)}, s32[64]{0:T(128)}, u32[]{:S(2)}) copy-start(s32[64]{0:T(128)} %param.29) | copy-start | bytes 772
  17.1 51.5 %copy-start.23 = (s32[64]{0:T(128)S(1)}, s32[64]{0:T(128)}, u32[]{:S(2)}) copy-start(s32[64]{0:T(128)} %param.27) | copy-start | bytes 772
  17.1 57.3 %copy-start.19 = (s32[64,32]{0,1:T(8,128)S(1)}, s32[64,32]{0,1:T(8,128)}, u32[]{:S(2)}) copy-start(s32[64,32]{0,1:T(8,128)} %param.28) | copy-start | bytes 24580
  56.6 52.6 %all-to-all-start.1 = ((bf16[2,64,64,128]{3,1,0,2:T(8,128)(2,1)}), bf16[2,64,64,128]{3,1,0,2:T(8,128)(2,1)S(1)}, u32[]{:S(2)}, u32[]{:S(2)}) async-start(bf16[2,64,64,128]{3,1,0,2:T(8,128)(2,1)} %copy.53), calls=%async_computation.1 | async-start | bytes 4194304 | tf_op jit(solution)/shard_map/all_to_all | solution.py:193
  66.7 69.0 %collective-permute-start = (bf16[1,4096,256]{2,1,0:T(8,128)(2,1)}, bf16[1,4096,256]{2,1,0:T(8,128)(2,1)}, u32[]{:S(2)}, u32[]{:S(2)}) collective-permute-start(bf16[1,4096,256]{2,1,0:T(8,128)(2,1)} %bitcast.305), channel_id=1, source_target_pairs={{0,1},{1,0},{2,3},{3,2},{4,5},{5,4},{6,7},{7,6},{8,9},{9,8},{10,11... | collective-permute-start | bytes 6291464 | tf_op jit(solution)/shard_map/ppermute | solution.py:39
  112.4 30.3 %copy-start.8 = (bf16[16,2,64,4,128]{4,2,1,0,3:T(8,128)(2,1)}, bf16[16,2,64,4,128]{4,2,1,0,3:T(8,128)(2,1)S(1)}, u32[]{:S(2)}) copy-start(bf16[16,2,64,4,128]{4,2,1,0,3:T(8,128)(2,1)S(1)} %copy.55) | copy-start | bytes 6291460
  112.4 23.3 %copy-start.11 = (bf16[256,16,256]{2,0,1:T(8,128)(2,1)S(1)}, bf16[256,16,256]{2,0,1:T(8,128)(2,1)}, u32[]{:S(2)}) copy-start(bf16[256,16,256]{2,0,1:T(8,128)(2,1)} %copy-done.10) | copy-start | bytes 6291460
  142.7 3.2 copy-start.6
  177.5 4.0 copy-start.1
  195.5 4.0 copy-start.1
  213.5 4.0 copy-start.1
  231.5 4.0 copy-start.1
  249.6 4.0 copy-start.1
  267.6 4.0 copy-start.1
  285.6 4.0 copy-start.1
  460.6 5.0 copy-start.18
  469.6 3.0 copy-start.2
  476.3 5.0 copy-start.18
  485.3 3.0 copy-start.2
  492.0 5.0 copy-start.18
  501.0 3.0 copy-start.2
  507.7 5.0 copy-start.18
  516.7 3.0 copy-start.2
  523.4 5.0 copy-start.18
  539.2 5.0 copy-start.18
  554.9 5.0 copy-start.18
  570.6 5.0 copy-start.18
  767.3 42.5 %copy-start.24 = (s32[32]{0:T(128)S(1)}, s32[32]{0:T(128)}, u32[]{:S(2)}) copy-start(s32[32]{0:T(128)} %get-tuple-element.2855) | copy-start | bytes 388
  812.0 5.0 copy-start.17
  821.0 3.0 copy-start.3
  827.7 5.0 copy-start.17
  836.7 3.0 copy-start.3
  848.1 8.7 collective-permute-start.1
  859.6 182.3 %collective-permute-start.2 = (bf16[1,2,64,4,128]{4,3,0,2,1:T(4,128)(2,1)}, bf16[1,2,64,4,128]{4,3,0,2,1:T(4,128)(2,1)}, u32[]{:S(2)}, u32[]{:S(2)}) collective-permute-start(bf16[1,2,64,4,128]{4,3,0,2,1:T(4,128)(2,1)} %get-tuple-element.2200), channel_id=1, source_target_pairs={{0,2},{1,3},{2,4},{3,5},{4,6},{5,7},{6,8},{7,9},{8,10},{9,11},{10,... | collective-permute-start | bytes 393224 | tf_op jit(solution)/shard_map/ppermute | solution.py:33
  869.1 180.4 %collective-permute-start.3 = (bf16[1,2,64,4,128]{4,3,0,2,1:T(4,128)(2,1)}, bf16[1,2,64,4,128]{4,3,0,2,1:T(4,128)(2,1)}, u32[]{:S(2)}, u32[]{:S(2)}) collective-permute-start(bf16[1,2,64,4,128]{4,3,0,2,1:T(4,128)(2,1)} %get-tuple-element.2199), channel_id=1, source_target_pairs={{0,3},{1,4},{2,5},{3,6},{4,7},{5,8},{6,9},{7,10},{8,11},{9,12},{10... | collective-permute-start | bytes 393224 | tf_op jit(solution)/shard_map/ppermute | solution.py:33
  1029.7 21.8 %collective-permute-start.4 = (bf16[1,2,64,4,128]{4,3,0,2,1:T(4,128)(2,1)}, bf16[1,2,64,4,128]{4,3,0,2,1:T(4,128)(2,1)S(1)}, u32[]{:S(2)}, u32[]{:S(2)}) collective-permute-start(bf16[1,2,64,4,128]{4,3,0,2,1:T(4,128)(2,1)} %get-tuple-element.2198), channel_id=1, source_target_pairs={{0,4},{1,5},{2,6},{3,7},{4,8},{5,9},{6,10},{7,11},{8,12},{9,13},{1... | collective-permute-start | bytes 393224 | tf_op jit(solution)/shard_map/ppermute | solution.py:33
  1041.4 14.0 %collective-permute-start.5 = (bf16[1,2,64,4,128]{4,3,0,2,1:T(4,128)(2,1)S(1)}, bf16[1,2,64,4,128]{4,3,0,2,1:T(4,128)(2,1)S(1)}, u32[]{:S(2)}, u32[]{:S(2)}) collective-permute-start(bf16[1,2,64,4,128]{4,3,0,2,1:T(4,128)(2,1)S(1)} %get-tuple-element.2197), channel_id=1, source_target_pairs={{0,5},{1,6},{2,7},{3,8},{4,9},{5,10},{6,11},{7,12},{8,13},{9,14},{... | collective-permute-start | bytes 393224 | tf_op jit(solution)/shard_map/ppermute | solution.py:33
  1041.9 23.2 %collective-permute-start.6 = (bf16[1,2,64,4,128]{4,3,0,2,1:T(4,128)(2,1)S(1)}, bf16[1,2,64,4,128]{4,3,0,2,1:T(4,128)(2,1)S(1)}, u32[]{:S(2)}, u32[]{:S(2)}) collective-permute-start(bf16[1,2,64,4,128]{4,3,0,2,1:T(4,128)(2,1)S(1)} %get-tuple-element.2196), channel_id=1, source_target_pairs={{0,6},{1,7},{2,8},{3,9},{4,10},{5,11},{6,12},{7,13},{8,14},{9,15},... | collective-permute-start | bytes 393224 | tf_op jit(solution)/shard_map/ppermute | solution.py:33
  1041.9 26.4 %collective-permute-start.7 = (bf16[1,2,64,4,128]{4,3,0,2,1:T(4,128)(2,1)S(1)}, bf16[1,2,64,4,128]{4,3,0,2,1:T(4,128)(2,1)S(1)}, u32[]{:S(2)}, u32[]{:S(2)}) collective-permute-start(bf16[1,2,64,4,128]{4,3,0,2,1:T(4,128)(2,1)S(1)} %get-tuple-element.2195), channel_id=1, source_target_pairs={{0,7},{1,8},{2,9},{3,10},{4,11},{5,12},{6,13},{7,14},{8,15},{9,0},... | collective-permute-start | bytes 393224 | tf_op jit(solution)/shard_map/ppermute | solution.py:33
  1049.5 22.3 %collective-permute-start.8 = (bf16[1,2,64,4,128]{4,3,0,2,1:T(4,128)(2,1)S(1)}, bf16[1,2,64,4,128]{4,3,0,2,1:T(4,128)(2,1)S(1)}, u32[]{:S(2)}, u32[]{:S(2)}) collective-permute-start(bf16[1,2,64,4,128]{4,3,0,2,1:T(4,128)(2,1)S(1)} %get-tuple-element.2194), channel_id=1, source_target_pairs={{0,8},{1,9},{2,10},{3,11},{4,12},{5,13},{6,14},{7,15},{8,0},{9,1},... | collective-permute-start | bytes 393224 | tf_op jit(solution)/shard_map/ppermute | solution.py:33
  1051.4 22.5 %collective-permute-start.9 = (bf16[1,2,64,4,128]{4,3,0,2,1:T(4,128)(2,1)S(1)}, bf16[1,2,64,4,128]{4,3,0,2,1:T(4,128)(2,1)S(1)}, u32[]{:S(2)}, u32[]{:S(2)}) collective-permute-start(bf16[1,2,64,4,128]{4,3,0,2,1:T(4,128)(2,1)S(1)} %get-tuple-element.2193), channel_id=1, source_target_pairs={{0,9},{1,10},{2,11},{3,12},{4,13},{5,14},{6,15},{7,0},{8,1},{9,2},... | collective-permute-start | bytes 393224 | tf_op jit(solution)/shard_map/ppermute | solution.py:33
  1055.4 22.7 %collective-permute-start.10 = (bf16[1,2,64,4,128]{4,3,0,2,1:T(4,128)(2,1)S(1)}, bf16[1,2,64,4,128]{4,3,0,2,1:T(4,128)(2,1)S(1)}, u32[]{:S(2)}, u32[]{:S(2)}) collective-permute-start(bf16[1,2,64,4,128]{4,3,0,2,1:T(4,128)(2,1)S(1)} %get-tuple-element.2192), channel_id=1, source_target_pairs={{0,10},{1,11},{2,12},{3,13},{4,14},{5,15},{6,0},{7,1},{8,2},{9,3},... | collective-permute-start | bytes 393224 | tf_op jit(solution)/shard_map/ppermute | solution.py:33
  1065.1 13.4 %collective-permute-start.11 = (bf16[1,2,64,4,128]{4,3,0,2,1:T(4,128)(2,1)S(1)}, bf16[1,2,64,4,128]{4,3,0,2,1:T(4,128)(2,1)S(1)}, u32[]{:S(2)}, u32[]{:S(2)}) collective-permute-start(bf16[1,2,64,4,128]{4,3,0,2,1:T(4,128)(2,1)S(1)} %get-tuple-element.2191), channel_id=1, source_target_pairs={{0,11},{1,12},{2,13},{3,14},{4,15},{5,0},{6,1},{7,2},{8,3},{9,4},{... | collective-permute-start | bytes 393224 | tf_op jit(solution)/shard_map/ppermute | solution.py:33
  1068.3 10.6 collective-permute-start.12
  1071.8 7.2 collective-permute-start.13
  1073.9 6.7 collective-permute-start.14
  1078.2 5.0 collective-permute-start.15
  (17 other events, 35.9 us)
